TPU v7x, 32 devices: a whole 2x2x4 slice. The times are simulated.
32 devices in a mesh: row: 4 (over y, x), col: 8 (over z, core).
Axes of the slice: x: 2, y: 2, z: 4, core: 2. Of those that a mesh axis runs over, the one named last changes fastest.
Arguments:
- basis: bfloat16 [40, 131072], P(None, ('row', 'col'))
- expand: float32 [3, 8, 40], replicated, may hold values from -1 to 1
- tiles: bfloat16 [3, 3072, 128, 128], P(None, ('row', 'col')), may hold values from -0.3125 to 0.3125
- tile_rows: int32 [3072], P(('row', 'col')), may hold values from 0 to 255, as said below
- tile_cols: int32 [3072], P(('row', 'col')), may hold values from 0 to 127
Outputs:
- new_block: float32 [8, 131072], P(None, ('row', 'col'))
- coefficients: float32 [8, 40], replicated
- factor: float32 [8, 8], replicated
Inputs may be any that keep to these rules, and one draw needn't show every extreme that they name: `tile_rows`: each device's 96 tiles come in 8 runs of 12; the row tiles of run k are 12 distinct values from k * 32 to (k + 1) * 32 - 1.
All inputs are finite; a program needn't handle non-finite values.
Results may differ from a plain program's by a relative error of at most 0.0054.
Values may be sent and summed in bfloat16 or wider, within the bound.
A program may use at most 64 MiB of HBM per device.

v0:
```python
import math
import jax
import jax.numpy as jnp
from jax import lax
from jax.sharding import PartitionSpec as P


def shards(basis, expand, tiles, tile_rows, tile_cols):
    highest = lax.Precision.HIGHEST
    row_count = lax.axis_size("row")
    col_count = lax.axis_size("col")
    krylov, length = basis.shape
    tile_size = tiles.shape[2]
    block_size = expand.shape[1]
    entries = length * row_count * col_count
    inverse_root = 1.0 / math.sqrt(entries)
    region = length // tile_size
    basis_full = basis.astype(jnp.float32)
    series = jnp.einsum("mbk,kn->mbn", expand, basis_full, precision=highest).astype(jnp.bfloat16)
    gathered = lax.all_gather(series, "row", axis=2, tiled=True)
    col_tiles = gathered.reshape(3, block_size, row_count * length // tile_size, tile_size)
    picked = jnp.take(col_tiles, tile_cols, axis=2)
    products = jnp.einsum("mtij,mbtj->bti", tiles, picked, preferred_element_type=jnp.float32)
    slot_count = col_count * region
    onehot = (tile_rows[:, None] == jnp.arange(slot_count, dtype=jnp.int32)[None, :]).astype(
        jnp.float32
    )
    partial_value = jnp.einsum("ts,bti->bsi", onehot, products, precision=highest).reshape(
        block_size, slot_count * tile_size
    )
    applied = lax.psum_scatter(partial_value, "col", scatter_dimension=1, tiled=True)
    raw_proj = jnp.dot(applied, basis_full.T, precision=highest) * inverse_root
    correlation = jnp.dot(basis_full, basis_full.T, precision=highest) / entries
    energy = jnp.dot(applied, applied.T, precision=highest)
    first_pass, correlation, energy = lax.psum((raw_proj, correlation, energy), ("row", "col"))
    second_pass = first_pass - jnp.dot(first_pass, correlation, precision=highest)
    coefficients = first_pass + second_pass
    mixed = jnp.dot(first_pass, coefficients.T, precision=highest)
    curved = jnp.dot(
        jnp.dot(coefficients, correlation, precision=highest), coefficients.T, precision=highest
    )
    gram_block = (energy - mixed - mixed.T + curved) / entries
    cleaned = applied - jnp.dot(coefficients, basis_full, precision=highest) * inverse_root
    factor = jnp.linalg.cholesky(gram_block)
    new_block = lax.linalg.triangular_solve(factor, cleaned, left_side=True, lower=True)
    return (new_block, coefficients, factor)


def solution(mesh):
    return jax.shard_map(
        shards,
        mesh=mesh,
        in_specs=(
            P(None, ("row", "col")),
            P(),
            P(None, ("row", "col"), None, None),
            P(("row", "col")),
            P(("row", "col")),
        ),
        out_specs=(P(None, ("row", "col")), P(), P()),
        check_vma=False,
    )
```

profile of v0, /device:TPU:10, one launch (start us, length us, event | category | flops | bytes accessed | tf_op | source)
XLA Modules:
  0.0 118.9 jit_solution(17451722167365213223)
XLA Ops:
  7.2 0.0 copy-start
  7.2 0.0 copy-start.2
  7.2 0.0 reduce-scatter.2.cloned.1.call-start
  7.2 0.7 compare_select_fusion
  7.9 0.7 compare_and_fusion
  8.6 0.0 copy-done
  8.6 1.0 convolution_convert_fusion
  9.6 11.2 %all_gather.3 = bf16[3,8,16384]{2,1,0:T(8,128)(2,1)S(1)} all-gather(bf16[3,8,4096]{2,1,0:T(8,128)(2,1)S(1)} %convolution_convert_fusion), channel_id=1, replica_groups=mesh['row'=4,'col'=8] {'row'}, dimensions={2}, use_global_device_ids=true | all-gather | bytes 983040 | tf_op jit(solution)/shard_map/all_gather | solution.py:20
  20.8 0.8 gather_fusion
  21.6 5.9 %fusion = f32[96,8,128,1]{2,1,3,0:T(8,128)S(1)} fusion(bf16[3,96,128,128]{3,2,1,0:T(8,128)(2,1)} %param.7, bf16[96,3,8,128]{3,2,1,0:T(8,128)(2,1)S(1)} %gather_fusion, pred[96]{0:T(512)(128)(4,1)S(1)} %compare_and_fusion), kind=kOutput, calls=%fused_computation.1 | convolution fusion | flops 75792384 | bytes 10420320 | tf_op jit(solution)/shard_map/mtij,mbtj->bti/dot_general | solution.py:23
  27.5 0.7 convolution_bitcast_fusion
  28.2 0.3 copy.13
  28.5 1.6 %copy.31 = f32[1,8,256,128]{3,1,2,0:T(8,128)} copy(f32[1,8,256,128]{3,2,1,0:T(8,128)S(1)} %bitcast.54) | data formatting | bytes 2097152
  30.1 0.0 reduce-scatter.2.cloned.1.call-update
  30.2 0.2 convolution_multiply_fusion.1
  30.4 29.0 %reduce-scatter.2.cloned.1.call-done = f32[8,4096]{1,0:T(8,128)} async-done(((f32[8,32768]{1,0:T(8,128)}), f32[8,4096]{1,0:T(8,128)}) %reduce-scatter.2.cloned.1.call-update) | async-done | bytes 131088 | tf_op jit(solution)/shard_map/reduce_scatter | solution.py:31
  59.4 1.3 %convolution_multiply_fusion.2 = f32[8,40]{1,0:T(8,128)S(1)} fusion(f32[8,4096]{1,0:T(8,128)} %reduce-scatter.2.cloned.1.call-done, bf16[40,4096]{1,0:T(8,128)(2,1)S(1)} %copy-done), kind=kOutput, calls=%fused_computation.12 | convolution fusion | flops 15728960 | bytes 460032 | tf_op jit(solution)/shard_map/dot_general | solution.py:32
  60.7 1.3 %fusion.19 = f32[8,8]{0,1:T(8,128)S(1)} fusion(f32[8,4096]{1,0:T(8,128)} %reduce-scatter.2.cloned.1.call-done), kind=kOutput, calls=%fused_computation.39 | convolution fusion | flops 3145728 | bytes 131328 | tf_op jit(solution)/shard_map/dot_general | solution.py:34
  62.0 43.9 %all-reduce = (f32[8,40]{1,0:T(8,128)S(1)}, f32[40,40]{1,0:T(8,128)S(1)}, f32[8,8]{0,1:T(8,128)S(1)}) all-reduce(f32[8,40]{1,0:T(8,128)S(1)} %convolution_multiply_fusion.2, f32[40,40]{1,0:T(8,128)S(1)} %convolution_multiply_fusion.1, f32[8,8]{0,1:T(8,128)S(1)} %fusion.19), channel_id=1, replica_groups=mesh['row'=4,'col'=8] {'row','col'}, use_global_device_ids=true, to_apply=%region_2.3 | all-reduce | flops 1984 | bytes 15872 | tf_op jit(solution)/shard_map/psum | solution.py:35
  105.9 0.1 fusion.3
  106.0 0.1 fusion.20
  106.2 0.1 fusion.21
  106.3 0.1 copy.15
  106.4 0.1 fusion.4
  106.5 0.1 copy.17
  106.6 0.7 cholesky.16
  107.3 0.1 select_reduce_fusion
  107.4 0.6 compare_reduce_fusion
  108.0 1.2 %select_bitcast_fusion = (f32[1,8,8]{2,1,0:T(8,128)S(1)}, f32[8,8]{1,0:T(8,128)}) fusion(f32[8,8]{1,0:T(8,128)S(1)} %cholesky.16, pred[]{:T(512)} %compare_reduce_fusion), kind=kLoop, calls=%fused_computation.30 | loop fusion | flops 256 | bytes 769 | tf_op jit(solution)/shard_map/triangular_solve | solution.py:45
  109.3 0.6 custom-call.6
  109.9 1.2 fusion.2
  111.1 1.0 fusion.15
  (5 shorter events, 0.0 us)
Async XLA Ops:
  7.2 1.4 %copy-start = (bf16[40,4096]{1,0:T(8,128)(2,1)S(1)}, bf16[40,4096]{1,0:T(8,128)(2,1)}, u32[]{:S(2)}) copy-start(bf16[40,4096]{1,0:T(8,128)(2,1)} %param.5) | copy-start | bytes 983044
  7.2 20.3 %copy-start.2 = (s32[96]{0:T(128)S(1)}, s32[96]{0:T(128)}, u32[]{:S(2)}) copy-start(s32[96]{0:T(128)} %param.8) | copy-start | bytes 1156
  7.2 52.2 %reduce-scatter.2.cloned.1.call-start = ((), (), s32[]{:S(2)}) async-start(), calls=%async_computation.1 | async-start | bytes 1179648 | tf_op jit(solution)/shard_map/reduce_scatter | solution.py:31
  106.0 6.0 %copy-start.1 = (f32[8,40]{1,0:T(8,128)}, f32[8,40]{1,0:T(8,128)S(1)}, u32[]{:S(2)}) copy-start(f32[8,40]{1,0:T(8,128)S(1)} %fusion.3) | copy-start | bytes 3844
Sparse Core Ops, SparseCore 0:
  30.3 29.0 reduce-scatter.1
where the time goes:
time: 119 us
  blocking collectives  55.1 us (46%)
  waiting for transfers between devices  29 us (24%)
  between operations  14.1 us (12%)
  matrix products  13.1 us (11%)
  other arithmetic  4.65 us (4%)
  local copies, waits for them, and re-layouts  2.88 us (2%)
    psum x1, blocking collectives, shards(): lax.psum((raw_proj, correlation, energy), ('row', 'col'))  43.9 us
    reduce_scatter x1, waiting for transfers between devices, shards(): lax.psum_scatter(partial_value, 'col', scatter_dimension=1, tiled=True)  29 us
    all_gather x1, blocking collectives, shards(): gathered = lax.all_gather(series, 'row', axis=2, tiled=True)  11.2 us
    dot_general x1, matrix products, shards(): jnp.einsum('mtij,mbtj->bti', tiles, picked, preferred_element_type=jnp.fl...  5.9 us
  transfers between devices with their start and end apart: 1, of which 1 were waited for; matrix products, arithmetic and copies ran while one was open for 0% of the time, Pallas kernels for 0%

commit v1 on v0

--- a/solution.py
+++ b/solution.py
@@ -17,7 +17,12 @@
     region = length // tile_size
     basis_full = basis.astype(jnp.float32)
     series = jnp.einsum("mbk,kn->mbn", expand, basis_full, precision=highest).astype(jnp.bfloat16)
-    gathered = lax.all_gather(series, "row", axis=2, tiled=True)
+    ring = [series]
+    for hop in range(3):
+        ring.append(lax.ppermute(ring[-1], "row", [(dev, (dev + 1) % 4) for dev in range(4)]))
+    gathered = jnp.roll(
+        jnp.concatenate(ring[::-1], axis=2), (lax.axis_index("row") + 1) * ring[0].shape[2], axis=2
+    )
     col_tiles = gathered.reshape(3, block_size, row_count * length // tile_size, tile_size)
     picked = jnp.take(col_tiles, tile_cols, axis=2)
     products = jnp.einsum("mtij,mbtj->bti", tiles, picked, preferred_element_type=jnp.float32)

time: 119 us -> 129 us (1.084)
  waiting for transfers between devices: 29 us -> 41.4 us
  blocking collectives: 55.1 us -> 43.8 us
  starting transfers between devices: 0.04 us -> 7.24 us
    all_gather x1 -> x0, blocking collectives: 11.2 us -> none  [shards(): gathered = lax.all_gather(series, 'row', axis=2, tiled=True)]
    ppermute x0 -> x3, waiting for transfers between devices: none -> 10.4 us  [shards(): lax.ppermute(ring[-1], 'row', [(dev, (dev + 1) % 4) for dev in range(4)])]
    ppermute x0 -> x3, starting transfers between devices: none -> 7.21 us  [shards(): lax.ppermute(ring[-1], 'row', [(dev, (dev + 1) % 4) for dev in range(4)])]
    reduce_scatter x1, waiting for transfers between devices: 29 us -> 31 us  [shards(): lax.psum_scatter(partial_value, 'col', scatter_dimension=1, tiled=True)]
    unnamed x7 -> x14, local copies, waits for them, and re-layouts: 1.62 us -> 2.65 us
  transfers between devices with their start and end apart: 1 -> 4, of which waited for: 1 -> 4; matrix products, arithmetic and copies ran while one was open for 0% -> 1% of each run, Pallas kernels for 0% -> 0%
where the time goes in v1:
time: 129 us; the launch traced here: 128 us
  blocking collectives  43.8 us (34%)
  waiting for transfers between devices  41.4 us (32%)
  between operations  14.2 us (11%)
  matrix products  13.1 us (10%)
  starting transfers between devices  7.24 us (6%)
  other arithmetic  4.61 us (4%)
  local copies, waits for them, and re-layouts  3.98 us (3%)
    psum x1, blocking collectives, shards(): lax.psum((raw_proj, correlation, energy), ('row', 'col'))  43.8 us
    reduce_scatter x1, waiting for transfers between devices, shards(): lax.psum_scatter(partial_value, 'col', scatter_dimension=1, tiled=True)  31 us
    ppermute x3, waiting for transfers between devices, shards(): lax.ppermute(ring[-1], 'row', [(dev, (dev + 1) % 4) for dev in range(4)])  10.4 us
    ppermute x3, starting transfers between devices, shards(): lax.ppermute(ring[-1], 'row', [(dev, (dev + 1) % 4) for dev in range(4)])  7.21 us
    dot_general x1, matrix products, shards(): jnp.einsum('mtij,mbtj->bti', tiles, picked, preferred_element_type=jnp.fl...  5.9 us
    unnamed x14, local copies, waits for them, and re-layouts  2.65 us
  transfers between devices with their start and end apart: 4, of which 4 were waited for; matrix products, arithmetic and copies ran while one was open for 1% of the time, Pallas kernels for 0%

profile of v1, /device:TPU:10, one launch (start us, length us, event | category | flops | bytes accessed | tf_op | source)
XLA Modules:
  0.0 128.4 jit_solution(3646461074901886381)
XLA Ops:
  7.2 0.9 copy-done
  8.1 1.0 convolution_convert_fusion
  9.2 1.5 %collective-permute-start = (bf16[3,8,4096]{2,1,0:T(8,128)(2,1)S(1)}, bf16[3,8,4096]{2,1,0:T(8,128)(2,1)S(1)}, u32[]{:S(2)}, u32[]{:S(2)}) collective-permute-start(bf16[3,8,4096]{2,1,0:T(8,128)(2,1)S(1)} %convolution_convert_fusion), channel_id=1, source_target_pairs={{0,8},{8,16},{16,24},{24,0},{1,9},{9,17},{17,25},{25,1},{2,10},{10... | collective-permute-start | bytes 589832 | tf_op jit(solution)/shard_map/ppermute | solution.py:22
  10.7 5.2 %collective-permute-done = bf16[3,8,4096]{2,1,0:T(8,128)(2,1)S(1)} collective-permute-done((bf16[3,8,4096]{2,1,0:T(8,128)(2,1)S(1)}, bf16[3,8,4096]{2,1,0:T(8,128)(2,1)S(1)}, u32[]{:S(2)}, u32[]{:S(2)}) %collective-permute-start) | collective-permute-done | bytes 196640 | tf_op jit(solution)/shard_map/ppermute | solution.py:22
  15.9 2.4 %collective-permute-start.1 = (bf16[3,8,4096]{2,1,0:T(8,128)(2,1)S(1)}, bf16[3,8,4096]{2,1,0:T(8,128)(2,1)S(1)}, u32[]{:S(2)}, u32[]{:S(2)}) collective-permute-start(bf16[3,8,4096]{2,1,0:T(8,128)(2,1)S(1)} %collective-permute-done), channel_id=1, source_target_pairs={{0,8},{8,16},{16,24},{24,0},{1,9},{9,17},{17,25},{25,1},{2,10},{10... | collective-permute-start | bytes 589832 | tf_op jit(solution)/shard_map/ppermute | solution.py:22
  18.2 0.7 compare_select_fusion
  18.9 2.7 %collective-permute-done.1 = bf16[3,8,4096]{2,1,0:T(8,128)(2,1)S(1)} collective-permute-done((bf16[3,8,4096]{2,1,0:T(8,128)(2,1)S(1)}, bf16[3,8,4096]{2,1,0:T(8,128)(2,1)S(1)}, u32[]{:S(2)}, u32[]{:S(2)}) %collective-permute-start.1) | collective-permute-done | bytes 196640 | tf_op jit(solution)/shard_map/ppermute | solution.py:22
  21.6 3.3 %collective-permute-start.2 = (bf16[3,8,4096]{2,1,0:T(8,128)(2,1)S(1)}, bf16[3,8,4096]{2,1,0:T(8,128)(2,1)S(1)}, u32[]{:S(2)}, u32[]{:S(2)}) collective-permute-start(bf16[3,8,4096]{2,1,0:T(8,128)(2,1)S(1)} %collective-permute-done.1), channel_id=1, source_target_pairs={{0,8},{8,16},{16,24},{24,0},{1,9},{9,17},{17,25},{25,1},{2,10},{10... | collective-permute-start | bytes 589832 | tf_op jit(solution)/shard_map/ppermute | solution.py:22
  24.9 0.7 compare_and_fusion
  25.6 2.5 %collective-permute-done.2 = bf16[3,8,4096]{2,1,0:T(8,128)(2,1)S(1)} collective-permute-done((bf16[3,8,4096]{2,1,0:T(8,128)(2,1)S(1)}, bf16[3,8,4096]{2,1,0:T(8,128)(2,1)S(1)}, u32[]{:S(2)}, u32[]{:S(2)}) %collective-permute-start.2) | collective-permute-done | bytes 196640 | tf_op jit(solution)/shard_map/ppermute | solution.py:22
  28.4 0.8 gather_fusion
  29.2 5.9 %fusion = f32[96,8,128,1]{2,1,3,0:T(8,128)S(1)} fusion(bf16[3,96,128,128]{3,2,1,0:T(8,128)(2,1)} %param.7, bf16[96,3,8,128]{3,2,1,0:T(8,128)(2,1)S(1)} %gather_fusion, pred[96]{0:T(512)(128)(4,1)S(1)} %compare_and_fusion), kind=kOutput, calls=%fused_computation.1 | convolution fusion | flops 75792384 | bytes 10420320 | tf_op jit(solution)/shard_map/mtij,mbtj->bti/dot_general | solution.py:28
  35.1 0.7 convolution_bitcast_fusion
  35.7 0.3 copy.13
  36.1 1.6 %copy.31 = f32[1,8,256,128]{3,1,2,0:T(8,128)} copy(f32[1,8,256,128]{3,2,1,0:T(8,128)S(1)} %bitcast.55) | data formatting | bytes 2097152
  37.7 0.2 convolution_multiply_fusion.1
  37.9 31.0 %reduce-scatter.2.cloned.1.call-done = f32[8,4096]{1,0:T(8,128)} async-done(((f32[8,32768]{1,0:T(8,128)}), f32[8,4096]{1,0:T(8,128)}) %reduce-scatter.2.cloned.1.call-update) | async-done | bytes 131088 | tf_op jit(solution)/shard_map/reduce_scatter | solution.py:36
  68.9 1.3 convolution_multiply_fusion.2
  70.2 1.3 %fusion.19 = f32[8,8]{0,1:T(8,128)S(1)} fusion(f32[8,4096]{1,0:T(8,128)} %reduce-scatter.2.cloned.1.call-done), kind=kOutput, calls=%fused_computation.48 | convolution fusion | flops 3145728 | bytes 131328 | tf_op jit(solution)/shard_map/dot_general | solution.py:39
  71.5 43.8 %all-reduce = (f32[8,40]{1,0:T(8,128)S(1)}, f32[40,40]{1,0:T(8,128)S(1)}, f32[8,8]{0,1:T(8,128)S(1)}) all-reduce(f32[8,40]{1,0:T(8,128)S(1)} %convolution_multiply_fusion.2, f32[40,40]{1,0:T(8,128)S(1)} %convolution_multiply_fusion.1, f32[8,8]{0,1:T(8,128)S(1)} %fusion.19), channel_id=1, replica_groups=mesh['row'=4,'col'=8] {'row','col'}, use_global_device_ids=true, to_apply=%region_2.3 | all-reduce | flops 1984 | bytes 15872 | tf_op jit(solution)/shard_map/psum | solution.py:40
  115.4 0.1 fusion.3
  115.5 0.1 fusion.21
  115.6 0.1 fusion.20
  115.8 0.1 copy.15
  115.8 0.1 fusion.4
  116.0 0.1 copy.17
  116.1 0.7 cholesky.16
  116.8 0.6 compare_reduce_fusion
  117.5 1.2 select_bitcast_fusion
  118.7 0.6 custom-call.6
  119.3 1.2 fusion.2
  120.5 1.0 fusion.15
  (19 shorter events, 0.3 us)
Async XLA Ops:
  7.2 1.0 copy-start
  7.2 61.7 %reduce-scatter.2.cloned.1.call-start = ((), (), s32[]{:S(2)}) async-start(), calls=%async_computation.1 | async-start | bytes 1179648 | tf_op jit(solution)/shard_map/reduce_scatter | solution.py:36
  9.2 6.7 %collective-permute-start = (bf16[3,8,4096]{2,1,0:T(8,128)(2,1)S(1)}, bf16[3,8,4096]{2,1,0:T(8,128)(2,1)S(1)}, u32[]{:S(2)}, u32[]{:S(2)}) collective-permute-start(bf16[3,8,4096]{2,1,0:T(8,128)(2,1)S(1)} %convolution_convert_fusion), channel_id=1, source_target_pairs={{0,8},{8,16},{16,24},{24,0},{1,9},{9,17},{17,25},{25,1},{2,10},{10... | collective-permute-start | bytes 589832 | tf_op jit(solution)/shard_map/ppermute | solution.py:22
  15.9 5.8 %collective-permute-start.1 = (bf16[3,8,4096]{2,1,0:T(8,128)(2,1)S(1)}, bf16[3,8,4096]{2,1,0:T(8,128)(2,1)S(1)}, u32[]{:S(2)}, u32[]{:S(2)}) collective-permute-start(bf16[3,8,4096]{2,1,0:T(8,128)(2,1)S(1)} %collective-permute-done), channel_id=1, source_target_pairs={{0,8},{8,16},{16,24},{24,0},{1,9},{9,17},{17,25},{25,1},{2,10},{10... | collective-permute-start | bytes 589832 | tf_op jit(solution)/shard_map/ppermute | solution.py:22
  21.6 6.5 %collective-permute-start.2 = (bf16[3,8,4096]{2,1,0:T(8,128)(2,1)S(1)}, bf16[3,8,4096]{2,1,0:T(8,128)(2,1)S(1)}, u32[]{:S(2)}, u32[]{:S(2)}) collective-permute-start(bf16[3,8,4096]{2,1,0:T(8,128)(2,1)S(1)} %collective-permute-done.1), channel_id=1, source_target_pairs={{0,8},{8,16},{16,24},{24,0},{1,9},{9,17},{17,25},{25,1},{2,10},{10... | collective-permute-start | bytes 589832 | tf_op jit(solution)/shard_map/ppermute | solution.py:22
  29.2 5.9 %copy-start.2 = (s32[96]{0:T(128)S(1)}, s32[96]{0:T(128)}, u32[]{:S(2)}) copy-start(s32[96]{0:T(128)} %param.8) | copy-start | bytes 1156
  115.5 6.0 %copy-start.1 = (f32[8,40]{1,0:T(8,128)}, f32[8,40]{1,0:T(8,128)S(1)}, u32[]{:S(2)}) copy-start(f32[8,40]{1,0:T(8,128)S(1)} %fusion.3) | copy-start | bytes 3844
Sparse Core Ops, SparseCore 0:
  37.8 31.0 reduce-scatter.1

commit v2 on v0

--- a/solution.py
+++ b/solution.py
@@ -32,7 +32,9 @@
     raw_proj = jnp.dot(applied, basis_full.T, precision=highest) * inverse_root
     correlation = jnp.dot(basis_full, basis_full.T, precision=highest) / entries
     energy = jnp.dot(applied, applied.T, precision=highest)
-    first_pass, correlation, energy = lax.psum((raw_proj, correlation, energy), ("row", "col"))
+    first_pass, correlation, energy = lax.psum(
+        lax.psum((raw_proj, correlation, energy), "row"), "col"
+    )
     second_pass = first_pass - jnp.dot(first_pass, correlation, precision=highest)
     coefficients = first_pass + second_pass
     mixed = jnp.dot(first_pass, coefficients.T, precision=highest)

time: 119 us -> 123 us (1.034)
  the two profiles are of different devices: /device:TPU:10 before, /device:TPU:0 now
where the time goes in v2:
time: 123 us
  blocking collectives  54.9 us (45%)
  waiting for transfers between devices  32.9 us (27%)
  between operations  14.1 us (11%)
  matrix products  13.1 us (11%)
  other arithmetic  4.65 us (4%)
  local copies, waits for them, and re-layouts  2.88 us (2%)
    reduce_scatter x1, waiting for transfers between devices, shards(): lax.psum_scatter(partial_value, 'col', scatter_dimension=1, tiled=True)  32.8 us
    psum x1, blocking collectives, shards(): lax.psum(lax.psum((raw_proj, correlation, energy), 'row'), 'col')  26 us
    psum x1, blocking collectives, shards(): lax.psum((raw_proj, correlation, energy), 'row')  16.2 us
    all_gather x1, blocking collectives, shards(): gathered = lax.all_gather(series, 'row', axis=2, tiled=True)  12.7 us
    dot_general x1, matrix products, shards(): jnp.einsum('mtij,mbtj->bti', tiles, picked, preferred_element_type=jnp.fl...  5.9 us
  transfers between devices with their start and end apart: 1, of which 1 were waited for; matrix products, arithmetic and copies ran while one was open for 0% of the time, Pallas kernels for 0%

profile of v2, /device:TPU:0, one launch (start us, length us, event | category | flops | bytes accessed | tf_op | source)
XLA Modules:
  0.0 122.5 jit_solution(9012022430855467745)
XLA Ops:
  7.2 0.0 copy-start
  7.2 0.0 reduce-scatter.2.cloned.1.call-start
  7.2 0.7 compare_select_fusion
  7.9 0.7 compare_and_fusion
  8.6 0.0 copy-done
  8.6 1.0 convolution_convert_fusion
  9.6 12.7 %all_gather.3 = bf16[3,8,16384]{2,1,0:T(8,128)(2,1)S(1)} all-gather(bf16[3,8,4096]{2,1,0:T(8,128)(2,1)S(1)} %convolution_convert_fusion), channel_id=1, replica_groups=mesh['row'=4,'col'=8] {'row'}, dimensions={2}, use_global_device_ids=true | all-gather | bytes 983040 | tf_op jit(solution)/shard_map/all_gather | solution.py:20
  22.3 0.8 gather_fusion
  23.1 5.9 %fusion = f32[96,8,128,1]{2,1,3,0:T(8,128)S(1)} fusion(bf16[3,96,128,128]{3,2,1,0:T(8,128)(2,1)} %param.7, bf16[96,3,8,128]{3,2,1,0:T(8,128)(2,1)S(1)} %gather_fusion, pred[96]{0:T(512)(128)(4,1)S(1)} %compare_and_fusion), kind=kOutput, calls=%fused_computation.1 | convolution fusion | flops 75792384 | bytes 10420320 | tf_op jit(solution)/shard_map/mtij,mbtj->bti/dot_general | solution.py:23
  29.0 0.7 convolution_bitcast_fusion
  29.7 0.3 copy.13
  30.0 1.6 %copy.31 = f32[1,8,256,128]{3,1,2,0:T(8,128)} copy(f32[1,8,256,128]{3,2,1,0:T(8,128)S(1)} %bitcast.54) | data formatting | bytes 2097152
  31.6 0.0 reduce-scatter.2.cloned.1.call-update
  31.6 0.2 convolution_multiply_fusion.1
  31.9 32.8 %reduce-scatter.2.cloned.1.call-done = f32[8,4096]{1,0:T(8,128)} async-done(((f32[8,32768]{1,0:T(8,128)}), f32[8,4096]{1,0:T(8,128)}) %reduce-scatter.2.cloned.1.call-update) | async-done | bytes 131088 | tf_op jit(solution)/shard_map/reduce_scatter | solution.py:31
  64.7 1.3 %convolution_multiply_fusion.2 = f32[8,40]{1,0:T(8,128)S(1)} fusion(f32[8,4096]{1,0:T(8,128)} %reduce-scatter.2.cloned.1.call-done, bf16[40,4096]{1,0:T(8,128)(2,1)S(1)} %copy-done), kind=kOutput, calls=%fused_computation.12 | convolution fusion | flops 15728960 | bytes 460032 | tf_op jit(solution)/shard_map/dot_general | solution.py:32
  66.0 1.3 %fusion.19 = f32[8,8]{0,1:T(8,128)S(1)} fusion(f32[8,4096]{1,0:T(8,128)} %reduce-scatter.2.cloned.1.call-done), kind=kOutput, calls=%fused_computation.39 | convolution fusion | flops 3145728 | bytes 131328 | tf_op jit(solution)/shard_map/dot_general | solution.py:34
  67.3 16.2 %all-reduce.1 = (f32[8,40]{1,0:T(8,128)S(1)}, f32[40,40]{1,0:T(8,128)S(1)}, f32[8,8]{0,1:T(8,128)S(1)}) all-reduce(f32[8,40]{1,0:T(8,128)S(1)} %convolution_multiply_fusion.2, f32[40,40]{1,0:T(8,128)S(1)} %convolution_multiply_fusion.1, f32[8,8]{0,1:T(8,128)S(1)} %fusion.19), channel_id=1, replica_groups=mesh['row'=4,'col'=8] {'row'}, use_global_device_ids=true, to_apply=%region_3.4 | all-reduce | flops 1984 | bytes 15872 | tf_op jit(solution)/shard_map/psum | solution.py:36
  83.5 26.0 %all-reduce = (f32[8,40]{1,0:T(8,128)S(1)}, f32[40,40]{1,0:T(8,128)S(1)}, f32[8,8]{0,1:T(8,128)S(1)}) all-reduce(f32[8,40]{1,0:T(8,128)S(1)} %get-tuple-element.6, f32[40,40]{1,0:T(8,128)S(1)} %get-tuple-element.7, f32[8,8]{0,1:T(8,128)S(1)} %get-tuple-element.8), channel_id=1, replica_groups=mesh['row'=4,'col'=8] {'col'}, use_global_device_ids=true, to_apply=%region_4.5 | all-reduce | flops 1984 | bytes 15872 | tf_op jit(solution)/shard_map/psum | solution.py:35
  109.5 0.1 fusion.3
  109.7 0.1 fusion.20
  109.8 0.1 fusion.21
  109.9 0.1 copy.15
  110.0 0.1 fusion.4
  110.2 0.1 copy.17
  110.2 0.7 cholesky.16
  110.9 0.1 select_reduce_fusion
  111.0 0.6 compare_reduce_fusion
  111.6 1.2 %select_bitcast_fusion = (f32[1,8,8]{2,1,0:T(8,128)S(1)}, f32[8,8]{1,0:T(8,128)}) fusion(f32[8,8]{1,0:T(8,128)S(1)} %cholesky.16, pred[]{:T(512)} %compare_reduce_fusion), kind=kLoop, calls=%fused_computation.30 | loop fusion | flops 256 | bytes 769 | tf_op jit(solution)/shard_map/triangular_solve | solution.py:47
  112.9 0.6 custom-call.6
  113.5 1.2 fusion.2
  114.7 1.0 fusion.15
  (6 shorter events, 0.0 us)
Async XLA Ops:
  7.2 1.4 %copy-start = (bf16[40,4096]{1,0:T(8,128)(2,1)S(1)}, bf16[40,4096]{1,0:T(8,128)(2,1)}, u32[]{:S(2)}) copy-start(bf16[40,4096]{1,0:T(8,128)(2,1)} %param.5) | copy-start | bytes 983044
  7.2 21.8 %copy-start.2 = (s32[96]{0:T(128)S(1)}, s32[96]{0:T(128)}, u32[]{:S(2)}) copy-start(s32[96]{0:T(128)} %param.8) | copy-start | bytes 1156
  7.2 57.5 %reduce-scatter.2.cloned.1.call-start = ((), (), s32[]{:S(2)}) async-start(), calls=%async_computation.1 | async-start | bytes 1179648 | tf_op jit(solution)/shard_map/reduce_scatter | solution.py:31
  109.7 6.0 %copy-start.1 = (f32[8,40]{1,0:T(8,128)}, f32[8,40]{1,0:T(8,128)S(1)}, u32[]{:S(2)}) copy-start(f32[8,40]{1,0:T(8,128)S(1)} %fusion.3) | copy-start | bytes 3844
Sparse Core Ops, SparseCore 0:
  31.8 32.8 reduce-scatter.1
